TPU v7x, 32 devices: a whole 2x2x4 slice. The times are simulated.
32 devices in a mesh: freq: 8 (over z, core), cell: 4 (over y, x).
Axes of the slice: x: 2, y: 2, z: 4, core: 2. Of those that a mesh axis runs over, the one named last changes fastest.
Arguments:
- covariance: bfloat16 [256, 2, 256, 256], P('freq', None, 'cell'), may hold values from -4 to 6, as said below
- replica: bfloat16 [256, 2, 256, 2048], P('freq', None, None, 'cell'), may hold values from -0.25 to 0.25
- transmission: bfloat16 [256, 2048], P('freq', 'cell'), may hold values from 0.29882812 to 3
Outputs:
- ambiguity: float32 [2048], P('cell')
- relative: float32 [2048], P('cell')
Inputs may be any that keep to these rules, and one draw needn't show every extreme that they name: Each covariance[f, 0] + i covariance[f, 1] is exactly Hermitian, also after rounding to bfloat16; before rounding all its eigenvalues are at least 0.5.
All inputs are finite; a program needn't handle non-finite values.
Results may differ from a plain program's by a relative error of at most 0.0003.
Values may be sent and summed in bfloat16 or wider, within the bound.
A program may use at most 384 MiB of HBM per device.

v0:
```python
import jax
import jax.numpy as jnp
from jax import lax
from jax.sharding import PartitionSpec as P


def quadratic(cov_piece, col_fields, row_fields):
    count, _, rows, depths = cov_piece.shape
    stacked = cov_piece.reshape(count, 2 * rows, depths)
    first = jnp.einsum(
        "fij,fjc->fic", stacked, col_fields[:, 0], preferred_element_type=jnp.float32
    )
    second = jnp.einsum(
        "fij,fjc->fic", stacked, col_fields[:, 1], preferred_element_type=jnp.float32
    )
    image_re = first[:, :rows] - second[:, rows:]
    image_im = first[:, rows:] + second[:, :rows]
    return jnp.sum(row_fields[:, 0] * image_re + row_fields[:, 1] * image_im, axis=1)


def shards(covariance, replica, transmission):
    freq_total = covariance.shape[0] * lax.axis_size("freq")
    power = quadratic(lax.all_gather(covariance, "cell", axis=2, tiled=True), replica, replica)
    amplitude = transmission.astype(jnp.float32)
    partial_value = jnp.sum(amplitude * amplitude * power, axis=0)
    partial_value = partial_value / jnp.float32(freq_total)
    ambiguity = lax.psum(partial_value, "freq")
    peak = lax.pmax(jnp.max(ambiguity), "cell")
    relative = ambiguity / jnp.maximum(peak, jnp.float32(1.0))
    return (ambiguity, relative)


def solution(mesh):
    return jax.shard_map(
        shards,
        mesh=mesh,
        in_specs=(P("freq", None, "cell", None), P("freq", None, None, "cell"), P("freq", "cell")),
        out_specs=(P("cell"), P("cell")),
        check_vma=False,
    )
```

profile of v0, /device:TPU:0, one launch (start us, length us, event | category | flops | bytes accessed | tf_op | source)
XLA Modules:
  0.0 197.6 jit_solution(6672672013921874193)
XLA Ops:
  7.2 0.0 all-gather.2.cloned.1.call-start
  7.2 0.7 all-gather.2.cloned.1.call-update
  7.9 92.2 %all-gather.2.cloned.1.call-done = bf16[32,2,256,256]{3,2,1,0:T(8,128)(2,1)} async-done(((bf16[32,2,64,256]{3,2,1,0:T(8,128)(2,1)}), bf16[32,2,256,256]{3,2,1,0:T(8,128)(2,1)}) %all-gather.2.cloned.1.call-update) | async-done | bytes 8388624 | tf_op jit(solution)/shard_map/all_gather | solution.py:23
  100.1 17.7 %fusion.4 = f32[32,512,512]{2,1,0:T(8,128)} fusion(bf16[32,512,256]{2,1,0:T(8,128)(2,1)} %bitcast.15, bf16[32,2,256,512]{3,2,1,0:T(8,128)(2,1)} %param.4), kind=kOutput, calls=%fused_computation.6 | convolution fusion | flops 4294967296 | bytes 50331648 | tf_op jit(solution)/shard_map/fij,fjc->fic/dot_general | solution.py:13
  117.8 17.7 %fusion.6 = f32[32,512,512]{2,1,0:T(8,128)} fusion(bf16[32,512,256]{2,1,0:T(8,128)(2,1)} %bitcast.16, bf16[32,2,256,512]{3,2,1,0:T(8,128)(2,1)} %param.4), kind=kOutput, calls=%fused_computation.8 | convolution fusion | flops 4294967296 | bytes 50331648 | tf_op jit(solution)/shard_map/fij,fjc->fic/dot_general | solution.py:10
  135.5 0.0 copy-start
  135.5 27.6 %fusion.2 = f32[32,512]{1,0:T(8,128)S(1)} fusion(f32[32,512,512]{2,1,0:T(8,128)} %fusion.4, f32[32,512,512]{2,1,0:T(8,128)} %fusion.6, bf16[32,2,256,512]{3,2,1,0:T(8,128)(2,1)} %param.4), kind=kLoop, calls=%fused_computation.3 | loop fusion | flops 33538048 | bytes 83951616 | tf_op jit(solution)/shard_map/reduce_sum | solution.py:18
  163.1 0.0 copy-done
  163.2 16.2 %psum.7 = f32[512]{0:T(512)S(1)} all-reduce(f32[512]{0:T(512)S(1)} %broadcast_multiply_fusion), channel_id=1, replica_groups=mesh['freq'=8,'cell'=4] {'freq'}, use_global_device_ids=true, to_apply=%region_2.0 | all-reduce | flops 512 | bytes 4096 | tf_op jit(solution)/shard_map/psum | solution.py:27
  179.4 0.0 copy-start.1
  179.4 0.6 reduce_max.9
  180.0 9.5 %pmax.7 = f32[]{:T(128)} all-reduce(f32[]{:T(128)} %reduce_max.9), channel_id=1, replica_groups=mesh['freq'=8,'cell'=4] {'cell'}, use_global_device_ids=true, to_apply=%region_4.0 | all-reduce | flops 1 | bytes 8 | tf_op jit(solution)/shard_map/pmax | solution.py:28
  190.2 0.6 broadcast_divide_fusion
  190.8 0.0 copy-done.1
  (2 shorter events, 0.0 us)
Async XLA Ops:
  7.2 92.9 %all-gather.2.cloned.1.call-start = ((), (), s32[]{:S(2)}) async-start(), calls=%async_computation | async-start | bytes 10485760 | tf_op jit(solution)/shard_map/all_gather | solution.py:23
  135.5 27.6 %copy-start = (bf16[32,512]{1,0:T(8,128)(2,1)S(1)}, bf16[32,512]{1,0:T(8,128)(2,1)}, u32[]{:S(2)}) copy-start(bf16[32,512]{1,0:T(8,128)(2,1)} %param.5) | copy-start | bytes 98308
  179.4 11.4 %copy-start.1 = (f32[512]{0:T(512)}, f32[512]{0:T(512)S(1)}, u32[]{:S(2)}) copy-start(f32[512]{0:T(512)S(1)} %psum.7) | copy-start | bytes 6148
Sparse Core Ops, SparseCore 0:
  9.8 90.1 all-gather.1
where the time goes:
time: 198 us
  waiting for transfers between devices  92.8 us (47%)
  matrix products  35.5 us (18%)
  other arithmetic  28.8 us (15%)
  blocking collectives  25.7 us (13%)
  between operations  14.7 us (7%)
    all_gather x1, waiting for transfers between devices, shards(): lax.all_gather(covariance, 'cell', axis=2, tiled=True)  92.2 us
    reduce_sum x1, other arithmetic, quadratic(): jnp.sum(row_fields[:, 0] * image_re + row_fields[:, 1] * image_im, axis=1)  27.6 us
    dot_general x1, matrix products, quadratic(): jnp.einsum('fij,fjc->fic', stacked, col_fields[:, 1], preferred_element_t...  17.7 us
    dot_general x1, matrix products, quadratic(): jnp.einsum('fij,fjc->fic', stacked, col_fields[:, 0], preferred_element_t...  17.7 us
    psum x1, blocking collectives, shards(): ambiguity = lax.psum(partial_value, 'freq')  16.2 us
    pmax x1, blocking collectives, shards(): peak = lax.pmax(jnp.max(ambiguity), 'cell')  9.54 us
  transfers between devices with their start and end apart: 1, of which 1 were waited for; matrix products, arithmetic and copies ran while one was open for 0% of the time, Pallas kernels for 0%

commit v1 on v0

--- a/solution.py
+++ b/solution.py
@@ -24,7 +24,11 @@
     amplitude = transmission.astype(jnp.float32)
     partial_value = jnp.sum(amplitude * amplitude * power, axis=0)
     partial_value = partial_value / jnp.float32(freq_total)
-    ambiguity = lax.psum(partial_value, "freq")
+    ambiguity = partial_value
+    for hop in (1, 2, 4):
+        ambiguity = ambiguity + lax.ppermute(
+            ambiguity, "freq", [(dev, dev ^ hop) for dev in range(8)]
+        )
     peak = lax.pmax(jnp.max(ambiguity), "cell")
     relative = ambiguity / jnp.maximum(peak, jnp.float32(1.0))
     return (ambiguity, relative)

time: 198 us -> 191 us (0.965)
  blocking collectives: 25.7 us -> 9.54 us
  waiting for transfers between devices: 92.8 us -> 98.2 us
  starting transfers between devices: 0.04 us -> 4 us
    psum x1 -> x0, blocking collectives: 16.2 us -> none  [shards(): ambiguity = lax.psum(partial_value, 'freq')]
    ppermute x0 -> x3, waiting for transfers between devices: none -> 5.33 us  [shards(): lax.ppermute(ambiguity, 'freq', [(dev, dev ^ hop) for dev in range(8)])]
    ppermute x0 -> x3, starting transfers between devices: none -> 3.96 us  [shards(): lax.ppermute(ambiguity, 'freq', [(dev, dev ^ hop) for dev in range(8)])]
  transfers between devices with their start and end apart: 1 -> 4, of which waited for: 1 -> 4; matrix products, arithmetic and copies ran while one was open for 0% -> 0% of each run, Pallas kernels for 0% -> 0%
where the time goes in v1:
time: 191 us
  waiting for transfers between devices  98.2 us (51%)
  matrix products  35.5 us (19%)
  other arithmetic  28.8 us (15%)
  between operations  14.7 us (8%)
  blocking collectives  9.54 us (5%)
  starting transfers between devices  4 us (2%)
    all_gather x1, waiting for transfers between devices, shards(): lax.all_gather(covariance, 'cell', axis=2, tiled=True)  92.2 us
    reduce_sum x1, other arithmetic, quadratic(): jnp.sum(row_fields[:, 0] * image_re + row_fields[:, 1] * image_im, axis=1)  27.6 us
    dot_general x1, matrix products, quadratic(): jnp.einsum('fij,fjc->fic', stacked, col_fields[:, 1], preferred_element_t...  17.7 us
    dot_general x1, matrix products, quadratic(): jnp.einsum('fij,fjc->fic', stacked, col_fields[:, 0], preferred_element_t...  17.7 us
    pmax x1, blocking collectives, shards(): peak = lax.pmax(jnp.max(ambiguity), 'cell')  9.54 us
    ppermute x3, waiting for transfers between devices, shards(): lax.ppermute(ambiguity, 'freq', [(dev, dev ^ hop) for dev in range(8)])  5.33 us
    ppermute x3, starting transfers between devices, shards(): lax.ppermute(ambiguity, 'freq', [(dev, dev ^ hop) for dev in range(8)])  3.96 us
  transfers between devices with their start and end apart: 4, of which 4 were waited for; matrix products, arithmetic and copies ran while one was open for 0% of the time, Pallas kernels for 0%

profile of v1, /device:TPU:0, one launch (start us, length us, event | category | flops | bytes accessed | tf_op | source)
XLA Modules:
  0.0 190.7 jit_solution(9695983650593079534)
XLA Ops:
  7.2 0.0 all-gather.2.cloned.1.call-start
  7.2 0.7 all-gather.2.cloned.1.call-update
  7.9 92.2 %all-gather.2.cloned.1.call-done = bf16[32,2,256,256]{3,2,1,0:T(8,128)(2,1)} async-done(((bf16[32,2,64,256]{3,2,1,0:T(8,128)(2,1)}), bf16[32,2,256,256]{3,2,1,0:T(8,128)(2,1)}) %all-gather.2.cloned.1.call-update) | async-done | bytes 8388624 | tf_op jit(solution)/shard_map/all_gather | solution.py:23
  100.1 17.7 %fusion.4 = f32[32,512,512]{2,1,0:T(8,128)} fusion(bf16[32,512,256]{2,1,0:T(8,128)(2,1)} %bitcast.15, bf16[32,2,256,512]{3,2,1,0:T(8,128)(2,1)} %param.4), kind=kOutput, calls=%fused_computation.6 | convolution fusion | flops 4294967296 | bytes 50331648 | tf_op jit(solution)/shard_map/fij,fjc->fic/dot_general | solution.py:13
  117.8 17.7 %fusion.6 = f32[32,512,512]{2,1,0:T(8,128)} fusion(bf16[32,512,256]{2,1,0:T(8,128)(2,1)} %bitcast.16, bf16[32,2,256,512]{3,2,1,0:T(8,128)(2,1)} %param.4), kind=kOutput, calls=%fused_computation.8 | convolution fusion | flops 4294967296 | bytes 50331648 | tf_op jit(solution)/shard_map/fij,fjc->fic/dot_general | solution.py:10
  135.5 0.0 copy-start
  135.5 27.6 %fusion.2 = f32[32,512]{1,0:T(8,128)S(1)} fusion(f32[32,512,512]{2,1,0:T(8,128)} %fusion.4, f32[32,512,512]{2,1,0:T(8,128)} %fusion.6, bf16[32,2,256,512]{3,2,1,0:T(8,128)(2,1)} %param.4), kind=kLoop, calls=%fused_computation.3 | loop fusion | flops 33538048 | bytes 83951616 | tf_op jit(solution)/shard_map/reduce_sum | solution.py:18
  163.1 0.0 copy-done
  163.2 0.1 collective-permute-start
  163.3 1.1 collective-permute-done
  164.4 1.5 collective-permute-start.1
  165.9 2.1 %collective-permute-done.1 = f32[512]{0:T(512)S(1)} collective-permute-done((f32[512]{0:T(512)S(1)}, f32[512]{0:T(512)S(1)}, u32[]{:S(2)}, u32[]{:S(2)}) %collective-permute-start.1) | collective-permute-done | bytes 2080 | tf_op jit(solution)/shard_map/ppermute | solution.py:29
  168.0 2.4 %collective-permute-start.2 = (f32[512]{0:T(512)S(1)}, f32[512]{0:T(512)S(1)}, u32[]{:S(2)}, u32[]{:S(2)}) collective-permute-start(f32[512]{0:T(512)S(1)} %add.18), channel_id=1, source_target_pairs={{0,16},{4,20},{8,24},{12,28},{16,0},{20,4},{24,8},{28,12},{1,17},{... | collective-permute-start | bytes 6152 | tf_op jit(solution)/shard_map/ppermute | solution.py:29
  170.4 2.1 %collective-permute-done.2 = f32[512]{0:T(512)S(1)} collective-permute-done((f32[512]{0:T(512)S(1)}, f32[512]{0:T(512)S(1)}, u32[]{:S(2)}, u32[]{:S(2)}) %collective-permute-start.2) | collective-permute-done | bytes 2080 | tf_op jit(solution)/shard_map/ppermute | solution.py:29
  172.5 0.6 fusion.11
  173.1 0.0 copy-start.1
  173.1 9.5 %pmax.7 = f32[]{:T(128)} all-reduce(f32[]{:T(128)} %get-tuple-element.2), channel_id=1, replica_groups=mesh['freq'=8,'cell'=4] {'cell'}, use_global_device_ids=true, to_apply=%region_3.0 | all-reduce | flops 1 | bytes 8 | tf_op jit(solution)/shard_map/pmax | solution.py:32
  183.3 0.6 broadcast_divide_fusion
  183.9 0.0 copy-done.1
  (4 shorter events, 0.0 us)
Async XLA Ops:
  7.2 92.9 %all-gather.2.cloned.1.call-start = ((), (), s32[]{:S(2)}) async-start(), calls=%async_computation | async-start | bytes 10485760 | tf_op jit(solution)/shard_map/all_gather | solution.py:23
  135.5 27.6 %copy-start = (bf16[32,512]{1,0:T(8,128)(2,1)S(1)}, bf16[32,512]{1,0:T(8,128)(2,1)}, u32[]{:S(2)}) copy-start(bf16[32,512]{1,0:T(8,128)(2,1)} %param.5) | copy-start | bytes 98308
  163.2 1.2 collective-permute-start
  164.4 3.6 %collective-permute-start.1 = (f32[512]{0:T(512)S(1)}, f32[512]{0:T(512)S(1)}, u32[]{:S(2)}, u32[]{:S(2)}) collective-permute-start(f32[512]{0:T(512)S(1)} %fusion.10), channel_id=1, source_target_pairs={{0,8},{4,12},{8,0},{12,4},{16,24},{20,28},{24,16},{28,20},{1,9},{5... | collective-permute-start | bytes 6152 | tf_op jit(solution)/shard_map/ppermute | solution.py:29
  168.0 4.5 %collective-permute-start.2 = (f32[512]{0:T(512)S(1)}, f32[512]{0:T(512)S(1)}, u32[]{:S(2)}, u32[]{:S(2)}) collective-permute-start(f32[512]{0:T(512)S(1)} %add.18), channel_id=1, source_target_pairs={{0,16},{4,20},{8,24},{12,28},{16,0},{20,4},{24,8},{28,12},{1,17},{... | collective-permute-start | bytes 6152 | tf_op jit(solution)/shard_map/ppermute | solution.py:29
  173.1 10.8 %copy-start.1 = (f32[512]{0:T(512)}, f32[512]{0:T(512)S(1)}, u32[]{:S(2)}) copy-start(f32[512]{0:T(512)S(1)} %get-tuple-element.3) | copy-start | bytes 6148
Sparse Core Ops, SparseCore 0:
  9.8 90.1 all-gather.1
